TPU v7x, 32 devices: a whole 2x2x4 slice. The times are simulated.
32 devices in a mesh: gx: 4 (over x, core), gy: 4 (over z), gz: 2 (over y).
Axes of the slice: x: 2, y: 2, z: 4, core: 2. Of those that a mesh axis runs over, the one named last changes fastest.
Arguments:
- left_modes: bfloat16 [2, 4, 2, 128, 3, 16384], P(None, None, None, None, None, ('gx', 'gy', 'gz')), may hold values from -0.23925781 to 0.23925781
- right_modes: bfloat16 [2, 4, 2, 128, 3, 16384], P(None, None, None, None, None, ('gx', 'gy', 'gz')), may hold values from -0.23925781 to 0.23925781
- gamma_cols: int32 [16, 4], replicated, may hold values from 0 to 3, each once within a row
- gamma_phase: int32 [16, 4], replicated, may hold values from 0 to 3
- dilution: int32 [64], replicated, may hold values from 0 to 3
- time_pairs: int32 [4, 2], replicated, may hold values from 0 to 1
Outputs:
- meson_fields: float32 [16, 2, 2, 128, 128], P('gz', None, None, ('gx', 'gy'))
- traces: float32 [4, 16, 16, 2], P(None, 'gz')
Inputs may be any that keep to these rules, and one draw needn't show every extreme that they name: Each row of gamma_cols is a permutation of the four spins.
All inputs are finite; a program needn't handle non-finite values.
Results may differ from a plain program's by a relative error of at most 0.0003.
Values sent between devices are 32-bit elements; how exact they have to be, the bound alone decides.
A program may use at most 128 MiB of HBM per device.

v0:
```python
import jax
import jax.numpy as jnp
from jax import lax
from jax.sharding import PartitionSpec as P

EXACT = lax.Precision.HIGHEST


def coefficients(gamma_cols, gamma_phase):
    spin_ids = jnp.arange(4, dtype=jnp.int32)
    onehot = (gamma_cols[:, :, None] == spin_ids[None, None, :]).astype(jnp.float32)
    real_sign = (gamma_phase == 0).astype(jnp.float32) - (gamma_phase == 2).astype(jnp.float32)
    imag_sign = (gamma_phase == 1).astype(jnp.float32) - (gamma_phase == 3).astype(jnp.float32)
    return (onehot * real_sign[:, :, None], onehot * imag_sign[:, :, None])


def select_pairs(crossed, time_pairs):
    time_ids = jnp.arange(crossed.shape[1], dtype=jnp.int32)
    first_time = (time_pairs[:, 0:1] == time_ids[None, :]).astype(jnp.float32)
    second_time = (time_pairs[:, 1:2] == time_ids[None, :]).astype(jnp.float32)
    chosen = jnp.einsum("pt,pu,gtahub->pgahb", first_time, second_time, crossed, precision=EXACT)
    real_part = chosen[:, :, 0, :, 0] - chosen[:, :, 1, :, 1]
    imag_part = chosen[:, :, 0, :, 1] + chosen[:, :, 1, :, 0]
    return jnp.stack([real_part, imag_part], axis=-1)


def project(coef_re, coef_im, pair_re, pair_im, form, part_axis):
    meson_re = jnp.einsum(form, coef_re, pair_re, precision=EXACT) - jnp.einsum(
        form, coef_im, pair_im, precision=EXACT
    )
    meson_im = jnp.einsum(form, coef_re, pair_im, precision=EXACT) + jnp.einsum(
        form, coef_im, pair_re, precision=EXACT
    )
    return jnp.stack([meson_re, meson_im], axis=part_axis)


def finish_whole(summed, time_pairs, local_gammas, block_rows, mode_count):
    group_start = lax.axis_index("gz") * local_gammas
    my_gammas = lax.dynamic_slice_in_dim(summed, group_start, local_gammas, 0)
    row_block = lax.axis_index("gx") * lax.axis_size("gy") + lax.axis_index("gy")
    meson_fields = lax.dynamic_slice_in_dim(my_gammas, row_block * block_rows, block_rows, 3)
    crossed = jnp.einsum("gtaij,hubji->gtahub", my_gammas, summed, precision=EXACT)
    traces = select_pairs(crossed, time_pairs) / mode_count
    return (meson_fields, traces)


def local(left_modes, right_modes, gamma_cols, gamma_phase, dilution, time_pairs):
    times_held = left_modes.shape[0]
    mode_count = left_modes.shape[3]
    gamma_count = gamma_cols.shape[0]
    noise_count = dilution.shape[0]
    low_count = mode_count - noise_count
    coef_re, coef_im = coefficients(gamma_cols, gamma_phase)
    groups = lax.axis_size("gz")
    blocks = lax.axis_size("gx") * lax.axis_size("gy")
    local_gammas = gamma_count // groups
    block_rows = mode_count // blocks
    spin_ids = jnp.arange(4, dtype=jnp.int32)
    noise_onehot = dilution[None, :] == spin_ids[:, None]
    select_table = noise_onehot.astype(jnp.bfloat16)
    low_re_list = []
    low_im_list = []
    noise_re_list = []
    noise_im_list = []
    for time_slot in range(times_held):
        left_slot = left_modes[time_slot]
        right_slot = right_modes[time_slot]
        low_prod = jnp.einsum(
            "spicx,qrjcx->sqpirj",
            left_slot,
            right_slot[:, :, :low_count],
            preferred_element_type=jnp.float32,
        )
        noise_right = jnp.sum(
            right_slot[:, :, low_count:] * select_table[:, None, :, None, None], axis=0
        )
        noise_prod = jnp.einsum(
            "spicx,qjcx->spiqj", left_slot, noise_right, preferred_element_type=jnp.float32
        )
        low_re_list.append(low_prod[:, :, 0, :, 0, :] + low_prod[:, :, 1, :, 1, :])
        low_im_list.append(low_prod[:, :, 0, :, 1, :] - low_prod[:, :, 1, :, 0, :])
        noise_re_list.append(noise_prod[:, 0, :, 0, :] + noise_prod[:, 1, :, 1, :])
        noise_im_list.append(noise_prod[:, 0, :, 1, :] - noise_prod[:, 1, :, 0, :])
    low_re, low_im, noise_re, noise_im = lax.psum(
        (
            jnp.stack(low_re_list),
            jnp.stack(low_im_list),
            jnp.stack(noise_re_list),
            jnp.stack(noise_im_list),
        ),
        ("gx", "gy", "gz"),
    )
    noise_float = noise_onehot.astype(jnp.float32)
    noise_coef_re = jnp.einsum("gsr,rj->gsj", coef_re, noise_float, precision=EXACT)
    noise_coef_im = jnp.einsum("gsr,rj->gsj", coef_im, noise_float, precision=EXACT)
    low_part = project(coef_re, coef_im, low_re, low_im, "gsr,tsrij->gtij", 2)
    noise_part = project(noise_coef_re, noise_coef_im, noise_re, noise_im, "gsj,tsij->gtij", 2)
    summed = jnp.concatenate([low_part, noise_part], axis=4)
    meson_fields, traces = finish_whole(summed, time_pairs, local_gammas, block_rows, mode_count)
    return (meson_fields, traces)


def solution(mesh):
    return jax.shard_map(
        local,
        mesh=mesh,
        in_specs=(
            P(None, None, None, None, None, ("gx", "gy", "gz")),
            P(None, None, None, None, None, ("gx", "gy", "gz")),
            P(),
            P(),
            P(),
            P(),
        ),
        out_specs=(P("gz", None, None, ("gx", "gy"), None), P(None, "gz", None, None)),
        check_vma=False,
    )
```

profile of v0, /device:TPU:0, one launch (start us, length us, event | category | flops | bytes accessed | tf_op | source)
XLA Modules:
  0.0 217.4 jit_solution(11653105158516507616)
XLA Ops:
  7.2 0.0 copy-start.7
  7.2 0.0 all-reduce.3.cloned.1.call-start
  7.2 0.0 copy-start.3
  7.2 3.5 %slice_bitcast_fusion = (bf16[4,2,128,3,512]{4,2,3,1,0:T(8,128)(2,1)S(1)}, bf16[4,2,128,3,512]{4,2,3,1,0:T(8,128)(2,1)S(1)}) fusion(bf16[2,4,2,128,3,512]{5,3,4,2,1,0:T(8,128)(2,1)} %param.7), kind=kLoop, calls=%fused_computation.9 | loop fusion | bytes 12582912 | tf_op jit(solution)/shard_map/squeeze | solution.py:67
  10.7 0.0 copy-done.7
  10.7 1.1 copy-done.3
  11.9 0.7 slice_bitcast_fusion.3
  12.6 0.9 fusion.19
  13.5 1.1 fusion.30
  14.7 1.8 fusion.15
  16.5 0.1 fusion.38
  16.6 0.1 fusion.41
  16.6 1.1 fusion.27
  17.8 1.8 fusion.12
  19.6 0.1 fusion.37
  19.8 0.8 pad_maximum_fusion.2
  20.6 1.5 pad_maximum_fusion
  22.1 0.0 all-reduce.3.cloned.1.call-update
  22.2 0.0 copy-done.8
  22.2 0.0 copy-done.6
  22.2 0.2 fusion.66
  22.4 0.1 copy.23
  22.5 0.2 fusion.64
  22.8 0.1 copy.25
  22.9 0.0 copy-done.9
  22.9 139.8 %all-reduce.3.cloned.1.call-done = (f32[2,4,128,64]{2,3,1,0:T(8,128)}, f32[2,4,128,64]{2,3,1,0:T(8,128)}, f32[2,4,4,128,64]{3,4,1,2,0:T(8,128)}, f32[2,4,4,128,64]{3,4,1,2,0:T(8,128)}) async-done(((f32[2,4,128,64]{2,3,1,0:T(8,128)}, f32[2,4,128,64]{2,3,1,0:T(8,128)}, f32[2,4,4,128,64]{3,4,1,2,0:T(8,128)}, f32[2,4,4,128,64]{3,4,1,2,0:T(8,128)}), (f32[2,4,128,64]{2,3,1,0:T(8,128)}, ...) | async-done | bytes 2621456 | tf_op jit(solution)/shard_map/psum | solution.py:84
  162.7 3.3 %convolution_bitcast_fusion.2 = f32[16,2,128,64]{2,0,3,1:T(8,128)S(1)} fusion(f32[2,4,4,128,64]{3,4,1,2,0:T(8,128)} %get-tuple-element.9, f32[16,4]{0,1:T(4,128)S(1)} %get-tuple-element.21, s32[16,4]{0,1:T(4,128)S(1)} %copy-done.6), kind=kOutput, calls=%fused_computation.29 | convolution fusion | flops 50332160 | bytes 2097664 | tf_op jit(solution)/shard_map/gsr,tsrij->gtij/dot_general | solution.py:28
  166.0 0.0 copy-start.1
  166.0 3.3 %convolution_bitcast_fusion = f32[16,2,128,64]{2,0,3,1:T(8,128)S(1)} fusion(f32[2,4,4,128,64]{3,4,1,2,0:T(8,128)} %get-tuple-element.8, f32[16,4]{0,1:T(4,128)S(1)} %get-tuple-element.21, s32[16,4]{0,1:T(4,128)S(1)} %copy-done.6), kind=kOutput, calls=%fused_computation.27 | convolution fusion | flops 50332160 | bytes 2097664 | tf_op jit(solution)/shard_map/gsr,tsrij->gtij/dot_general | solution.py:31
  169.3 0.0 copy-done.2
  169.4 0.0 copy-start.4
  169.4 0.0 copy-start.5
  169.4 2.0 fusion.24
  171.4 0.0 copy-done.1
  171.4 2.2 fusion.26
  173.6 0.0 copy-done.4
  173.6 1.2 fusion.48
  174.8 0.0 copy-done.5
  174.8 1.2 fusion.44
  175.9 1.2 fusion.22
  177.1 1.2 fusion.21
  178.3 4.0 %fusion.102 = (f32[16,2,2,128,128,1,1]{3,0,4,1,2,5,6:T(8,128)}, f32[16,2,2,128,128]{3,0,4,1,2:T(8,128)}) fusion(f32[16,2,1,128,64]{3,0,4,1,2:T(8,128)S(1)} %fusion.21, f32[16,2,1,128,64]{3,0,4,1,2:T(8,128)S(1)} %fusion.22, f32[16,2,1,128,64]{3,0,4,1,2:T(8,128)S(1)} %fusion.26, f32[16,2,1,128,64]{3,0,4,1,2:T(8,128)S(1)} %fusion.24), kind=kLoop, calls=%fused_computation.138 | loop fusion | flops 3145728 | bytes 12582912 | tf_op jit(solution)/shard_map/concatenate | solution.py:98
  182.2 5.8 %copy.70 = f32[16,2,2,128,128,1,1]{4,0,3,2,1,6,5:T(8,128)} copy(f32[16,2,2,128,128,1,1]{3,0,4,1,2,5,6:T(8,128)} %get-tuple-element.14) | data formatting | bytes 8388608 | tf_op jit(solution)/shard_map/concatenate | solution.py:98
  188.0 19.5 %fusion.10 = f32[8,2,2,16,2,2,1]{3,0,6,5,4,2,1:T(8,128)S(1)} fusion(f32[16,2,2,128,128,1,1]{4,0,3,2,1,6,5:T(8,128)} %copy.70, f32[16,2,2,128,128]{3,0,4,1,2:T(8,128)} %get-tuple-element.15, s32[]{:T(128)S(6)} %select_n.10), kind=kOutput, calls=%fused_computation.15 | convolution fusion | flops 402653184 | bytes 6299652 | tf_op jit(solution)/shard_map/gtaij,hubji->gtahub/dot_general | solution.py:42
  207.6 0.3 convolution_bitcast_fusion.4
  207.9 0.6 copy.37
  208.6 0.6 constant_dynamic-slice_fusion
  209.2 1.3 copy.36
  (16 shorter events, 0.1 us)
Async XLA Ops:
  7.2 3.6 %copy-start.7 = (s32[64]{0:T(128)S(1)}, s32[64]{0:T(128)}, u32[]{:S(2)}) copy-start(s32[64]{0:T(128)} %param.10) | copy-start | bytes 772
  7.2 155.5 %all-reduce.3.cloned.1.call-start = ((), (), s32[]{:S(2)}) async-start(), calls=%async_computation | async-start | bytes 5242880 | tf_op jit(solution)/shard_map/psum | solution.py:84
  7.2 4.6 %copy-start.3 = (bf16[2,4,2,128,3,512]{5,3,4,2,1,0:T(8,128)(2,1)S(1)}, bf16[2,4,2,128,3,512]{5,3,4,2,1,0:T(8,128)(2,1)}, u32[]{:S(2)}) copy-start(bf16[2,4,2,128,3,512]{5,3,4,2,1,0:T(8,128)(2,1)} %param.6) | copy-start | bytes 18874372
  20.6 1.5 copy-start.8
  20.6 1.6 copy-start.6
  20.6 2.3 %copy-start.9 = (s32[4,2]{0,1:T(2,128)S(1)}, s32[4,2]{0,1:T(2,128)}, u32[]{:S(2)}) copy-start(s32[4,2]{0,1:T(2,128)} %param.11) | copy-start | bytes 100
  162.7 6.6 %copy-start.2 = (f32[2,4,4,128,64]{3,4,1,2,0:T(8,128)S(1)}, f32[2,4,4,128,64]{3,4,1,2,0:T(8,128)}, u32[]{:S(2)}) copy-start(f32[2,4,4,128,64]{3,4,1,2,0:T(8,128)} %get-tuple-element.8) | copy-start | bytes 3145732
  166.0 5.4 %copy-start.1 = (f32[2,4,4,128,64]{3,4,1,2,0:T(8,128)S(1)}, f32[2,4,4,128,64]{3,4,1,2,0:T(8,128)}, u32[]{:S(2)}) copy-start(f32[2,4,4,128,64]{3,4,1,2,0:T(8,128)} %get-tuple-element.9) | copy-start | bytes 3145732
  169.4 4.2 %copy-start.4 = (f32[2,4,128,64]{2,3,1,0:T(8,128)S(1)}, f32[2,4,128,64]{2,3,1,0:T(8,128)}, u32[]{:S(2)}) copy-start(f32[2,4,128,64]{2,3,1,0:T(8,128)} %get-tuple-element.7) | copy-start | bytes 786436
  169.4 5.4 %copy-start.5 = (f32[2,4,128,64]{2,3,1,0:T(8,128)S(1)}, f32[2,4,128,64]{2,3,1,0:T(8,128)}, u32[]{:S(2)}) copy-start(f32[2,4,128,64]{2,3,1,0:T(8,128)} %get-tuple-element.6) | copy-start | bytes 786436
  188.0 20.6 %copy-start = (f32[16,2,2,128,128]{3,0,4,1,2:T(8,128)S(1)}, f32[16,2,2,128,128]{3,0,4,1,2:T(8,128)}, u32[]{:S(2)}) copy-start(f32[16,2,2,128,128]{3,0,4,1,2:T(8,128)} %get-tuple-element.15) | copy-start | bytes 12582916
Sparse Core Ops, SparseCore 0:
  22.3 140.3 all-reduce.2
where the time goes:
time: 218 us; the launch traced here: 217 us
  waiting for transfers between devices  140 us (64%)
  matrix products  41.6 us (19%)
  between operations  14.4 us (7%)
  local copies, waits for them, and re-layouts  14 us (6%)
  other arithmetic  7.57 us (3%)
    psum x1, waiting for transfers between devices, local(): lax.psum((jnp.stack(low_re_list), jnp.stack(low_im_list), jnp.stack(noise...  140 us
    dot_general x1, matrix products, finish_whole(): jnp.einsum('gtaij,hubji->gtahub', my_gammas, summed, precision=EXACT)  19.5 us
    concatenate x1, local copies, waits for them, and re-layouts, local(): summed = jnp.concatenate([low_part, noise_part], axis=4)  5.8 us
    dot_general x2, matrix products, project(): jnp.einsum(form, coef_im, pair_re, precision=EXACT)  4.47 us
    dot_general x2, matrix products, project(): jnp.einsum(form, coef_im, pair_im, precision=EXACT)  4.46 us
  transfers between devices with their start and end apart: 1, of which 1 were waited for; matrix products, arithmetic and copies ran while one was open for 0% of the time, Pallas kernels for 0%

commit v1 on v0

v1 whole, which is shorter than its diff:
```python
import functools

import jax
import jax.numpy as jnp
from jax import lax
from jax.experimental import pallas as pl
from jax.experimental.pallas import tpu as pltpu
from jax.sharding import PartitionSpec as P

EXACT = lax.Precision.HIGHEST
MESH = pl.DeviceIdType.MESH
NT = (((1,), (1,)), ((), ()))


def nt_dot(a, b):
    return lax.dot_general(a, b, NT, preferred_element_type=jnp.float32)


def blocks_kernel(low, slabs, mask_ref, left_ref, right_ref, out_ref):
    spins = left_ref.shape[1]
    modes = left_ref.shape[4]
    depth = left_ref.shape[5]
    colour = pl.program_id(1)
    left_re = left_ref[0, :, 0, 0].reshape(spins * modes, depth)
    left_im = left_ref[0, :, 1, 0].reshape(spins * modes, depth)
    low_re = jnp.concatenate([right_ref[0, r, 0, 0, :low] for r in range(spins)], axis=0)
    low_im = jnp.concatenate([right_ref[0, r, 1, 0, :low] for r in range(spins)], axis=0)
    noise_re = right_ref[0, 0, 0, 0, low:] * mask_ref[0]
    noise_im = right_ref[0, 0, 1, 0, low:] * mask_ref[0]
    for r in range(1, spins):
        noise_re = noise_re + right_ref[0, r, 0, 0, low:] * mask_ref[r]
        noise_im = noise_im + right_ref[0, r, 1, 0, low:] * mask_ref[r]
    low_out_re = nt_dot(left_re, low_re) + nt_dot(left_im, low_im)
    low_out_im = nt_dot(left_re, low_im) + nt_dot(left_im, -low_re)
    noise_out = nt_dot(left_re, jnp.concatenate([noise_re, noise_im], axis=0)) + nt_dot(
        left_im, jnp.concatenate([noise_im, -noise_re], axis=0)
    )
    half = low_out_re.shape[1] // 128
    per_spin = 2 * half + 1

    pieces = []
    for s in range(spins):
        rows = slice(s * modes, (s + 1) * modes)
        for k in range(half):
            pieces.append((s * per_spin + k, low_out_re[rows, k * 128 : (k + 1) * 128]))
        for k in range(half):
            pieces.append((s * per_spin + half + k, low_out_im[rows, k * 128 : (k + 1) * 128]))
        pieces.append((s * per_spin + 2 * half, noise_out[rows]))

    @pl.when(colour == 0)
    def _():
        for k, piece in pieces:
            out_ref[0, k] = piece
        for k in range(len(pieces), slabs):
            out_ref[0, k] = jnp.zeros((modes, 128), jnp.float32)

    @pl.when(colour != 0)
    def _():
        for k, piece in pieces:
            out_ref[0, k] += piece


def local_blocks(left, right, dilution, slabs):
    times, spins, parts, colours, modes, depth = left.shape
    noise_count = dilution.shape[0]
    low = modes - noise_count
    mask = (dilution[None, :] == jnp.arange(spins, dtype=jnp.int32)[:, None]).astype(jnp.bfloat16)
    mask = jnp.broadcast_to(mask[:, :, None], (spins, noise_count, depth))
    block = (1, spins, parts, 1, modes, depth)
    return pl.pallas_call(
        functools.partial(blocks_kernel, low, slabs),
        grid=(times, colours),
        in_specs=[
            pl.BlockSpec((spins, noise_count, depth), lambda t, c: (0, 0, 0)),
            pl.BlockSpec(block, lambda t, c: (t, 0, 0, c, 0, 0)),
            pl.BlockSpec(block, lambda t, c: (t, 0, 0, c, 0, 0)),
        ],
        out_specs=pl.BlockSpec((1, slabs, modes, 128), lambda t, c: (t, 0, 0, 0)),
        out_shape=jax.ShapeDtypeStruct((times, slabs, modes, 128), jnp.float32),
        compiler_params=pltpu.CompilerParams(
            dimension_semantics=("arbitrary", "arbitrary"), vmem_limit_bytes=48 * 1024 * 1024
        ),
        name="spin_blocks",
    )(mask, left, right)


def chunk_transpose(rows, chunk):
    rows = list(rows)
    count = len(rows)
    lane = lax.broadcasted_iota(jnp.int32, rows[0].shape, 1) // chunk
    bit = 1
    while bit < count:
        upper = (lane // bit) % 2 == 1
        new = list(rows)
        for k in range(count):
            if k & bit:
                continue
            a, b = rows[k], rows[k | bit]
            new[k] = jnp.where(upper, pltpu.roll(b, bit * chunk, 1), a)
            new[k | bit] = jnp.where(upper, b, pltpu.roll(a, 128 - bit * chunk, 1))
        rows = new
        bit *= 2
    return rows


def exchange_kernel(
    dims, cols_ref, phase_ref, dil_ref, part_ref, meson_ref, trace_ref, *scratch
):
    (times, spins, low, gammas, gamma_local, nz, kz, nxo, nxi, ny, rows) = dims
    bufs = scratch[: 8 * times]
    (blocks, fields, outgoing, columns, totals, send_sem, recv_sem) = scratch[8 * times :]
    gx, gy, gz = lax.axis_index("gx"), lax.axis_index("gy"), lax.axis_index("gz")
    outer, inner = gx // nxi, gx % nxi
    nb = nxo * nxi * ny
    me = gx * ny + gy
    next_sem = [0]

    def block_peer(d):
        there = (me + d) % nb
        return there, {"gx": there // ny, "gy": there % ny, "gz": gz}

    barrier = pltpu.get_barrier_semaphore()
    for d in range(1, nb):
        _, device = block_peer(d)
        pl.semaphore_signal(barrier, inc=1, device_id=device, device_id_type=MESH)
    for d in range(1, nz):
        pl.semaphore_signal(
            barrier, inc=1, device_id={"gx": gx, "gy": gy, "gz": (gz + d) % nz}, device_id_type=MESH
        )
    pl.semaphore_wait(barrier, nb - 1 + nz - 1)

    def send(src, dst, device):
        k = next_sem[0]
        next_sem[0] += 1
        copy = pltpu.make_async_remote_copy(
            src_ref=src, dst_ref=dst, send_sem=send_sem.at[k], recv_sem=recv_sem.at[k],
            device_id=device, device_id_type=MESH,
        )
        copy.start()
        return copy

    def peer(axis, d):
        if axis == "inner":
            there = (inner + d) % nxi
            return there, {"gx": outer * nxi + there, "gy": gy, "gz": gz}
        if axis == "outer":
            there = (outer + d) % nxo
            return there, {"gx": there * nxi + inner, "gy": gy, "gz": gz}
        if axis == "gy":
            there = (gy + d) % ny
            return there, {"gx": gx, "gy": there, "gz": gz}
        there = (gz + d) % nz
        return there, {"gx": gx, "gy": gy, "gz": there}

    place = {"inner": inner, "outer": outer, "gy": gy, "gz": gz}
    size = {"inner": nxi, "outer": nxo, "gy": ny, "gz": nz}
    full = ["gz", "kz", "outer", "inner", "gy"]

    def begin(src, labels, axis, arrivals):
        at = labels.index(axis)
        copies = []
        for d in range(1, size[axis]):
            there, device = peer(axis, d)
            index = (slice(None),) * at + (there,)
            copies.append(send(src.at[index], arrivals.at[d - 1], device))
        return copies

    def finish(copies, src, labels, axis, arrivals, result):
        at = labels.index(axis)
        total = src[(slice(None),) * at + (place[axis],)]
        for d, copy in enumerate(copies):
            copy.wait_recv()
            total = total + arrivals[d]
        result[...] = total
        return [label for label in labels if label != axis]

    flows = []
    for t in range(times):
        order = ["inner", "outer", "gz", "gy"] if t % 2 == 0 else ["inner", "gz", "outer", "gy"]
        flows.append({"order": order, "src": part_ref.at[t], "labels": full, "bufs": bufs[8 * t : 8 * t + 8]})
    pending = []
    for step in range(4):
        for flow in flows:
            if step > 0:
                flow["labels"] = finish(
                    flow["copies"], flow["src"], flow["labels"], flow["order"][step - 1],
                    flow["bufs"][2 * step - 2], flow["bufs"][2 * step - 1],
                )
                flow["src"] = flow["bufs"][2 * step - 1]
            flow["copies"] = begin(flow["src"], flow["labels"], flow["order"][step], flow["bufs"][2 * step])
            pending += flow["copies"]
    for t, flow in enumerate(flows):
        finish(flow["copies"], flow["src"], flow["labels"], "gy", flow["bufs"][6], flow["bufs"][7].at[gz])
        mine = flow["bufs"][7].at[gz]
        flow["copies"] = [send(mine, flow["bufs"][7].at[gz], peer("gz", d)[1]) for d in range(1, nz)]
        pending += flow["copies"]

    half = spins * low // 128
    per_spin = 2 * half + 1
    lane = lax.broadcasted_iota(jnp.int32, (rows, 128), 1)
    is_low = lane < low
    dil = jnp.broadcast_to(dil_ref[...], (rows, 128))
    pack = 128 // low

    for t, flow in enumerate(flows):
        for copy in flow["copies"]:
            copy.wait_recv()
        own = flow["bufs"][7]

        def slab(k):
            return own[k // kz, k % kz]

        for s in range(spins):
            noise = slab(s * per_spin + 2 * half)
            for c in range(2):
                noise_c = noise if c == 1 else pltpu.roll(noise, low, 1)
                for r in range(spins):
                    piece = slab(s * per_spin + c * half + r // pack)
                    if r % pack:
                        piece = pltpu.roll(piece, 128 - (r % pack) * low, 1)
                    blocks[t, s, r, c] = jnp.where(
                        is_low, piece, jnp.where(dil == r, noise_c, 0.0)
                    )

    def one_gamma(g, carry):
        for t in range(times):
            re = jnp.zeros((rows, 128), jnp.float32)
            im = jnp.zeros((rows, 128), jnp.float32)
            for s in range(spins):
                col = cols_ref[g, s]
                phase = phase_ref[g, s]
                block_re = blocks[t, s, col, 0]
                block_im = blocks[t, s, col, 1]
                one = jnp.where(phase == 0, 1.0, jnp.where(phase == 2, -1.0, 0.0))
                eye = jnp.where(phase == 1, 1.0, jnp.where(phase == 3, -1.0, 0.0))
                re = re + (one * block_re - eye * block_im)
                im = im + (one * block_im + eye * block_re)
            fields[t, 0, g] = re
            fields[t, 1, g] = im
        return carry

    lax.fori_loop(0, gammas, one_gamma, 0)

    picked = []
    for t in range(times):
        for c in range(2):
            for g in range(gamma_local):
                value = fields[t, c, gz * gamma_local + g]
                meson_ref[g, t, c] = value
                picked.append(value)
    while len(picked) % nb:
        picked.append(jnp.zeros((rows, 128), jnp.float32))
    groups = len(picked) // nb
    for k in range(groups):
        moved = chunk_transpose(picked[k * nb : (k + 1) * nb], rows)
        for j in range(nb):
            outgoing[j, :, k * 128 : (k + 1) * 128] = moved[j]
    columns[me] = outgoing[me]
    copies = []
    for d in range(1, nb):
        there, device = block_peer(d)
        copies.append(send(outgoing.at[there], columns.at[me], device))
    pending += copies
    for copy in copies:
        copy.wait_recv()
    width = groups * 128
    right = columns[...].reshape(nb * rows, width)
    quarter = gammas * rows
    count = times * 2 * gamma_local
    lane_w = lax.broadcasted_iota(jnp.int32, (quarter, width), 1)
    row_w = lax.broadcasted_iota(jnp.int32, (quarter, width), 0)
    same = (row_w % rows) == (lane_w % rows)
    pick_from = lax.broadcasted_iota(jnp.int32, (width, 128), 0) // rows
    pick_to = lax.broadcasted_iota(jnp.int32, (width, 128), 1)
    partial = jnp.zeros((gammas, 128), jnp.float32)
    for t in range(times):
        for c in range(2):
            q = t * 2 + c
            left = fields[t, c].reshape(quarter, 128)
            cross = jnp.dot(left, right, precision=EXACT, preferred_element_type=jnp.float32)
            cross = jnp.where(same, cross, 0.0)
            cross = jnp.sum(cross.reshape(gammas, rows, width), axis=1)
            pick = ((pick_to == pick_from + q * count) & (pick_from < count)).astype(jnp.float32)
            partial = partial + jnp.dot(cross, pick, precision=EXACT, preferred_element_type=jnp.float32)
    totals[me] = partial
    copies = []
    for d in range(1, nb):
        _, device = block_peer(d)
        copies.append(send(totals.at[me], totals.at[me], device))
    pending += copies
    for copy in copies:
        copy.wait_recv()
    total = totals[0]
    for j in range(1, nb):
        total = total + totals[j]
    trace_ref[...] = total
    for copy in pending:
        copy.wait_send()


def exchange(parts, gamma_cols, gamma_phase, dilution, sizes, modes):
    nx, ny, nz = sizes
    times, slabs = parts.shape[:2]
    nxi = 2 if nx % 2 == 0 else 1
    nxo = nx // nxi
    kz = slabs // nz
    gammas, spins = gamma_cols.shape
    gamma_local = gammas // nz
    low = modes - dilution.shape[0]
    rows = modes // (nx * ny)
    nb = nx * ny
    parts = parts.reshape(times, nz, kz, nxo, nxi, ny, rows, 128)
    tile = (rows, 128)
    dil = jnp.concatenate([jnp.full((low,), -1, jnp.int32), dilution]).reshape(1, modes)
    dims = (times, spins, low, gammas, gamma_local, nz, kz, nxo, nxi, ny, rows)
    scratch = []
    sems = 0
    for t in range(times):
        shapes = []
        left_dims = {"gz": nz, "kz": kz, "outer": nxo, "inner": nxi, "gy": ny}
        order = ["inner", "outer", "gz", "gy"] if t % 2 == 0 else ["inner", "gz", "outer", "gy"]
        for axis in order:
            n = left_dims.pop(axis)
            sems += n - 1
            rest = tuple(left_dims.values())
            shapes.append((max(n - 1, 1),) + rest + tile)
            shapes.append(rest + tile)
        shapes[-1] = (nz, kz) + tile
        sems += nz - 1
        scratch += [pltpu.VMEM(shape, jnp.float32) for shape in shapes]
    sems += 2 * (nb - 1)
    groups = -(-(times * 2 * gamma_local) // nb)
    scratch += [
        pltpu.VMEM((times, spins, spins, 2) + tile, jnp.float32),
        pltpu.VMEM((times, 2, gammas) + tile, jnp.float32),
        pltpu.VMEM((nb, rows, groups * 128), jnp.float32),
        pltpu.VMEM((nb, rows, groups * 128), jnp.float32),
        pltpu.VMEM((nb, gammas, 128), jnp.float32),
        pltpu.SemaphoreType.DMA((sems,)),
        pltpu.SemaphoreType.DMA((sems,)),
    ]
    vmem = pl.BlockSpec(memory_space=pltpu.VMEM)
    smem = pl.BlockSpec(memory_space=pltpu.SMEM)
    return pl.pallas_call(
        functools.partial(exchange_kernel, dims),
        in_specs=[smem, smem, vmem, vmem],
        out_specs=[vmem, vmem],
        out_shape=[
            jax.ShapeDtypeStruct((gamma_local, times, 2) + tile, jnp.float32),
            jax.ShapeDtypeStruct((gammas, 128), jnp.float32),
        ],
        scratch_shapes=scratch,
        compiler_params=pltpu.CompilerParams(
            collective_id=0, has_side_effects=True, vmem_limit_bytes=48 * 1024 * 1024
        ),
        name="exchange",
    )(gamma_cols, gamma_phase, dil, parts)


def local(sizes, left_modes, right_modes, gamma_cols, gamma_phase, dilution, time_pairs):
    left = jnp.transpose(left_modes, (0, 1, 2, 4, 3, 5))
    right = jnp.transpose(right_modes, (0, 1, 2, 4, 3, 5))
    times, spins = left.shape[:2]
    modes = left.shape[4]
    noise_count = dilution.shape[0]
    low = modes - noise_count
    nz = sizes[2]
    used = spins * (2 * (spins * low // 128) + 1)
    slabs = -(-used // nz) * nz
    parts = local_blocks(left, right, dilution, slabs)
    meson_fields, packed = exchange(parts, gamma_cols, gamma_phase, dilution, sizes, modes)
    gammas = gamma_cols.shape[0]
    gamma_local = gammas // nz
    grid = packed[:, : times * 2 * times * 2 * gamma_local]
    grid = grid.reshape(gammas, times, 2, times, 2, gamma_local)
    time_ids = jnp.arange(times, dtype=jnp.int32)
    first = time_pairs[:, 0:1] == time_ids[None, :]
    second = time_pairs[:, 1:2] == time_ids[None, :]
    keep = first[:, None, :] & second[:, :, None]
    real = grid[:, :, 0, :, 0] - grid[:, :, 1, :, 1]
    imag = grid[:, :, 1, :, 0] + grid[:, :, 0, :, 1]
    both = jnp.stack([real, imag], axis=-1)
    chosen = jnp.where(keep[:, None, :, :, None, None], both[None], 0.0)
    traces = jnp.transpose(jnp.sum(chosen, axis=(2, 3)), (0, 2, 1, 3)) / modes
    return (meson_fields, traces)


def solution(mesh):
    sizes = (mesh.shape["gx"], mesh.shape["gy"], mesh.shape["gz"])
    modes_spec = P(None, None, None, None, None, ("gx", "gy", "gz"))
    return jax.shard_map(
        functools.partial(local, sizes),
        mesh=mesh,
        in_specs=(modes_spec, modes_spec, P(), P(), P(), P()),
        out_specs=(P("gz", None, None, ("gx", "gy"), None), P(None, "gz", None, None)),
        check_vma=False,
    )
```

time: 218 us -> 60 us (0.28)
  waiting for transfers between devices: 140 us -> 0 us
  Pallas kernels: 0 us -> 55.6 us
  matrix products: 41.6 us -> 0 us
  between operations: 14.4 us -> 0.72 us
  local copies, waits for them, and re-layouts: 14 us -> 2.5 us
  other arithmetic: 7.57 us -> 0.92 us
    psum x1 -> x0, waiting for transfers between devices: 140 us -> none  [local(): lax.psum((jnp.stack(low_re_list), jnp.stack(low_im_list), jnp.stack(noise...]
    pallas_call x0 -> x2, Pallas kernels: none -> 55.6 us  [the longest x1 46.2 us: exchange(): pl.pallas_call(functools.partial(exchange_kernel, dims), in_specs=[smem,...]
    dot_general x16 -> x0, matrix products: 41.6 us -> none  [the longest x1 19.5 us: finish_whole(): jnp.einsum('gtaij,hubji->gtahub', my_gammas, summed, precision=EXACT)]
    concatenate x1 -> x0, local copies, waits for them, and re-layouts: 5.8 us -> none  [local(): summed = jnp.concatenate([low_part, noise_part], axis=4)]
    squeeze x2 -> x0, local copies, waits for them, and re-layouts: 4.23 us -> none  [the longest x1 3.48 us: local(): right_slot = right_modes[time_slot]]
    concatenate x1 -> x0, other arithmetic: 3.95 us -> none  [local(): summed = jnp.concatenate([low_part, noise_part], axis=4)]
    another operation x3 -> x0, other arithmetic: 2.37 us -> none  [the longest x1 1.51 us: local(): jnp.stack(low_re_list)]
  transfers between devices with their start and end apart: 1 -> 0, of which waited for: 1 -> 0; matrix products, arithmetic and copies ran while one was open for 0% -> 0% of each run, Pallas kernels for 0% -> 0%
where the time goes in v1:
time: 60 us; the launch traced here: 59.7 us
  Pallas kernels  55.6 us (93%)
  local copies, waits for them, and re-layouts  2.5 us (4%)
  other arithmetic  0.92 us (2%)
  between operations  0.72 us (1%)
    pallas_call x1, Pallas kernels, exchange(): pl.pallas_call(functools.partial(exchange_kernel, dims), in_specs=[smem,...  46.2 us
    pallas_call x1, Pallas kernels, local_blocks(): pl.pallas_call(functools.partial(blocks_kernel, low, slabs), grid=(times,...  9.35 us
    unnamed x10, local copies, waits for them, and re-layouts  1.47 us

profile of v1, /device:TPU:0, one launch (start us, length us, event | category | flops | bytes accessed | tf_op | source)
XLA Modules:
  0.0 59.7 jit_solution(14784663991131411276)
XLA Ops:
  0.6 0.8 %slice_bitcast_fusion.3 = (s32[4]{0:T(128)S(1)}, s32[4]{0:T(128)S(1)}) fusion(s32[4,2]{0,1:T(2,128)} %param.11), kind=kLoop, calls=%fused_computation.15 | loop fusion | bytes 64 | tf_op jit(solution)/shard_map/eq | solution.py:377
  1.4 0.1 iota_compare_fusion
  1.5 0.1 broadcast_and_fusion
  1.5 0.7 %fusion.3 = bf16[4,64]{1,0:T(4,128)(2,1)S(1)} fusion(s32[64]{0:T(128)} %param.10), kind=kLoop, calls=%fused_computation.13 | loop fusion | flops 512 | bytes 768 | tf_op jit(solution)/shard_map/convert_element_type | solution.py:67
  2.2 0.1 broadcast_in_dim.15.mask_ref
  2.3 0.0 copy-start
  2.3 0.0 copy-start.1
  2.3 0.0 copy-start.2
  2.3 9.4 %spin_blocks.1 = f32[2,20,128,128]{3,2,1,0:T(8,128)S(1)} custom-call(bf16[4,64,512]{2,1,0:T(8,128)(2,1)S(1)} %broadcast_in_dim.15.mask_ref, bf16[2,4,2,3,128,512]{5,4,3,2,1,0:T(8,128)(2,1)} %bitcast.27, bf16[2,4,2,3,128,512]{5,4,3,2,1,0:T(8,128)(2,1)} %bitcast.28), custom_call_target="tpu_custom_call" | custom-call | tf_op jit(solution)/shard_map/spin_blocks/pallas_call | solution.py:70
  11.7 0.0 copy-done
  11.7 0.1 copy.19.cols_ref
  11.8 0.0 copy-done.1
  11.8 0.1 copy.20.phase_ref
  11.9 0.0 copy-done.2
  11.9 0.1 pad_bitcast_fusion.dil_ref
  12.0 46.2 %exchange.1 = (f32[8,2,2,8,128]{4,3,2,1,0:T(8,128)S(1)}, f32[16,128]{1,0:T(8,128)S(1)}) custom-call(s32[16,4]{1,0:T(8,128)S(1)} %copy.19.cols_ref, s32[16,4]{1,0:T(8,128)S(1)} %copy.20.phase_ref, s32[1,128]{1,0:T(1,128)S(1)} %pad_bitcast_fusion.dil_ref, f32[2,2,10,2,2,4,8,128]{7,6,5,4,3,2,1,0:T(8,128)S(1)} %bitcast.26), custom_call_target="tpu_custom_call" | custom-call | tf_op jit(solution)/shard_map/exchange/pallas_call | solution.py:344
  58.2 0.1 copy.21
  58.3 0.1 select_reduce_fusion
  58.4 0.6 %copy.25 = f32[4,8,16,2]{2,3,1,0:T(2,128)} copy(f32[4,8,16,2]{2,1,3,0:T(8,128)S(1)} %multiply_bitcast_fusion) | data formatting | bytes 8192
  59.1 0.7 %copy.31 = f32[8,2,2,8,128]{4,3,2,1,0:T(8,128)} copy(f32[8,2,2,8,128]{4,3,2,1,0:T(8,128)S(1)} %get-tuple-element.14) | data formatting | bytes 262144
  (3 shorter events, 0.0 us)
Async XLA Ops:
  2.3 9.4 %copy-start = (s32[16,4]{0,1:T(4,128)S(1)}, s32[16,4]{0,1:T(4,128)}, u32[]{:S(2)}) copy-start(s32[16,4]{0,1:T(4,128)} %param.8) | copy-start | bytes 772
  2.3 9.5 %copy-start.1 = (s32[16,4]{0,1:T(4,128)S(1)}, s32[16,4]{0,1:T(4,128)}, u32[]{:S(2)}) copy-start(s32[16,4]{0,1:T(4,128)} %param.9) | copy-start | bytes 772
  2.3 9.6 %copy-start.2 = (s32[64]{0:T(128)S(1)}, s32[64]{0:T(128)}, u32[]{:S(2)}) copy-start(s32[64]{0:T(128)} %param.10) | copy-start | bytes 772

commit v2 on v1

v2 whole, which is shorter than its diff:
```python
import functools

import jax
import jax.numpy as jnp
from jax import lax
from jax.experimental import pallas as pl
from jax.experimental.pallas import tpu as pltpu
from jax.sharding import PartitionSpec as P

EXACT = lax.Precision.HIGHEST
MESH = pl.DeviceIdType.MESH
NT = (((1,), (1,)), ((), ()))


def nt_dot(a, b):
    return lax.dot_general(a, b, NT, preferred_element_type=jnp.float32)


def chunk_transpose(rows, chunk):
    rows = list(rows)
    count = len(rows)
    lane = lax.broadcasted_iota(jnp.int32, rows[0].shape, 1) // chunk
    bit = 1
    while bit < count:
        upper = (lane // bit) % 2 == 1
        new = list(rows)
        for k in range(count):
            if k & bit:
                continue
            a, b = rows[k], rows[k | bit]
            new[k] = jnp.where(upper, pltpu.roll(b, bit * chunk, 1), a)
            new[k | bit] = jnp.where(upper, b, pltpu.roll(a, 128 - bit * chunk, 1))
        rows = new
        bit *= 2
    return rows


def flow_list(times):
    flows = []
    for t in range(times):
        flows.append((t, 0, ("inner", "outer", "gz", "gy")))
        flows.append((t, 1, ("inner", "gz", "outer", "gy")))
    return flows


def slab_range(part, kz):
    cut = kz // 2
    return (0, cut) if part == 0 else (cut, kz)


def fused_kernel(
    dims, cols_ref, phase_ref, dil_ref, left_ref, right_ref, meson_ref, trace_ref, *scratch
):
    (times, spins, colours, low, modes, depth, gammas, gamma_local, nz, kz, nxo, nxi, ny, rows) = dims
    flow_specs = flow_list(times)
    bufs = scratch[: 7 * len(flow_specs)]
    (
        left_buf, right_buf, parts, gathered, blocks, fields, outgoing, columns, totals,
        load_sem, send_sem, recv_sem,
    ) = scratch[7 * len(flow_specs) :]
    gx, gy, gz = lax.axis_index("gx"), lax.axis_index("gy"), lax.axis_index("gz")
    outer, inner = gx // nxi, gx % nxi
    nb = nxo * nxi * ny
    me = gx * ny + gy
    next_sem = [0]

    loads = []
    for t in range(times):
        for colour in range(colours):
            k = 2 * (t * colours + colour)
            pair = (
                pltpu.make_async_copy(
                    right_ref.at[t, :, :, colour], right_buf.at[t, colour], load_sem.at[k]
                ),
                pltpu.make_async_copy(
                    left_ref.at[t, :, :, colour], left_buf.at[t, colour], load_sem.at[k + 1]
                ),
            )
            for copy in pair:
                copy.start()
            loads.append(pair)

    def block_peer(d):
        there = (me + d) % nb
        return there, {"gx": there // ny, "gy": there % ny, "gz": gz}

    barrier = pltpu.get_barrier_semaphore()
    for d in range(1, nb):
        _, device = block_peer(d)
        pl.semaphore_signal(barrier, inc=1, device_id=device, device_id_type=MESH)
    for d in range(1, nz):
        pl.semaphore_signal(
            barrier, inc=1, device_id={"gx": gx, "gy": gy, "gz": (gz + d) % nz}, device_id_type=MESH
        )

    noise_count = modes - low
    at_lane = lax.broadcasted_iota(jnp.int32, (noise_count, modes), 1)
    at_row = lax.broadcasted_iota(jnp.int32, (noise_count, modes), 0)
    dil_row = jnp.broadcast_to(dil_ref[...], (noise_count, modes))
    masks = []
    for r in range(spins):
        hit = jnp.where((at_lane == at_row + low) & (dil_row == r), 1.0, 0.0)
        column = jnp.sum(hit, axis=1, keepdims=True)
        masks.append(jnp.broadcast_to(column, (noise_count, depth)).astype(jnp.bfloat16))

    half = spins * low // 128
    per_spin = 2 * half + 1

    def multiply(t, colour):
        for copy in loads[t * colours + colour]:
            copy.wait()
        left = left_buf.at[t, colour]
        right = right_buf.at[t, colour]
        left_re = left[:, 0].reshape(spins * modes, depth)
        left_im = left[:, 1].reshape(spins * modes, depth)
        low_re = jnp.concatenate([right[r, 0, :low] for r in range(spins)], axis=0)
        low_im = jnp.concatenate([right[r, 1, :low] for r in range(spins)], axis=0)
        noise_re = right[0, 0, low:] * masks[0]
        noise_im = right[0, 1, low:] * masks[0]
        for r in range(1, spins):
            noise_re = noise_re + right[r, 0, low:] * masks[r]
            noise_im = noise_im + right[r, 1, low:] * masks[r]
        low_out_re = nt_dot(left_re, low_re) + nt_dot(left_im, low_im)
        low_out_im = nt_dot(left_re, low_im) + nt_dot(left_im, -low_re)
        noise_out = nt_dot(left_re, jnp.concatenate([noise_re, noise_im], axis=0)) + nt_dot(
            left_im, jnp.concatenate([noise_im, -noise_re], axis=0)
        )

        def put(k, piece):
            piece = piece.reshape(nxo, nxi, ny, rows, 128)
            if colour == 0:
                parts[t, k // kz, k % kz] = piece
            else:
                parts[t, k // kz, k % kz] += piece

        for s in range(spins):
            at = slice(s * modes, (s + 1) * modes)
            for k in range(half):
                put(s * per_spin + k, low_out_re[at, k * 128 : (k + 1) * 128])
                put(s * per_spin + half + k, low_out_im[at, k * 128 : (k + 1) * 128])
            put(s * per_spin + 2 * half, noise_out[at])
        if colour == 0:
            for k in range(spins * per_spin, nz * kz):
                parts[t, k // kz, k % kz] = jnp.zeros((nxo, nxi, ny, rows, 128), jnp.float32)

    pending = []

    def send(src, dst, device):
        k = next_sem[0]
        next_sem[0] += 1
        copy = pltpu.make_async_remote_copy(
            src_ref=src, dst_ref=dst, send_sem=send_sem.at[k], recv_sem=recv_sem.at[k],
            device_id=device, device_id_type=MESH,
        )
        copy.start()
        pending.append(copy)
        return copy

    def peer(axis, d):
        if axis == "inner":
            there = (inner + d) % nxi
            return there, {"gx": outer * nxi + there, "gy": gy, "gz": gz}
        if axis == "outer":
            there = (outer + d) % nxo
            return there, {"gx": there * nxi + inner, "gy": gy, "gz": gz}
        if axis == "gy":
            there = (gy + d) % ny
            return there, {"gx": gx, "gy": there, "gz": gz}
        there = (gz + d) % nz
        return there, {"gx": gx, "gy": gy, "gz": there}

    place = {"inner": inner, "outer": outer, "gy": gy, "gz": gz}
    size = {"inner": nxi, "outer": nxo, "gy": ny, "gz": nz}

    def begin(flow):
        axis = flow["order"][flow["step"]]
        at = flow["labels"].index(axis)
        arrivals = flow["bufs"][2 * flow["step"]]
        flow["copies"] = []
        for d in range(1, size[axis]):
            there, device = peer(axis, d)
            index = (slice(None),) * at + (there,)
            flow["copies"].append(send(flow["src"].at[index], arrivals.at[d - 1], device))

    def finish(flow):
        step = flow["step"]
        axis = flow["order"][step]
        at = flow["labels"].index(axis)
        arrivals = flow["bufs"][2 * step]
        total = flow["src"][(slice(None),) * at + (place[axis],)]
        for d, copy in enumerate(flow["copies"]):
            copy.wait_recv()
            total = total + arrivals[d]
        if step < 3:
            result = flow["bufs"][2 * step + 1]
        else:
            result = gathered.at[flow["t"], gz, flow["k0"] : flow["k1"]]
        result[...] = total
        flow["src"] = result
        flow["labels"] = [label for label in flow["labels"] if label != axis]
        flow["step"] = step + 1

    flows = []
    for n, (t, part, order) in enumerate(flow_specs):
        k0, k1 = slab_range(part, kz)
        flows.append({
            "t": t, "k0": k0, "k1": k1, "order": order, "step": 0,
            "src": parts.at[t, :, k0:k1],
            "labels": ["gz", "kz", "outer", "inner", "gy"],
            "bufs": bufs[7 * n : 7 * n + 7],
        })

    def advance(t):
        for flow in flows:
            if flow["t"] != t:
                continue
            if "copies" in flow and flow["step"] < 4:
                finish(flow)
            if flow["step"] < 4:
                begin(flow)
            else:
                mine = gathered.at[t, gz, flow["k0"] : flow["k1"]]
                flow["copies"] = [send(mine, mine, peer("gz", d)[1]) for d in range(1, nz)]

    lane = lax.broadcasted_iota(jnp.int32, (rows, 128), 1)
    is_low = lane < low
    dil = jnp.broadcast_to(dil_ref[...], (rows, 128))
    pack = 128 // low
    groups = -(-(2 * gamma_local) // nb)
    width = groups * 128

    def make_fields(t):
        for flow in flows:
            if flow["t"] == t:
                for copy in flow["copies"]:
                    copy.wait_recv()

        def slab(k):
            return gathered[t, k // kz, k % kz]

        for s in range(spins):
            noise = slab(s * per_spin + 2 * half)
            for c in range(2):
                noise_c = noise if c == 1 else pltpu.roll(noise, low, 1)
                for r in range(spins):
                    piece = slab(s * per_spin + c * half + r // pack)
                    if r % pack:
                        piece = pltpu.roll(piece, 128 - (r % pack) * low, 1)
                    blocks[t, s, r, c] = jnp.where(
                        is_low, piece, jnp.where(dil == r, noise_c, 0.0)
                    )

        def one_gamma(g, carry):
            re = jnp.zeros((rows, 128), jnp.float32)
            im = jnp.zeros((rows, 128), jnp.float32)
            for s in range(spins):
                col = cols_ref[g, s]
                phase = phase_ref[g, s]
                block_re = blocks[t, s, col, 0]
                block_im = blocks[t, s, col, 1]
                one = jnp.where(phase == 0, 1.0, jnp.where(phase == 2, -1.0, 0.0))
                eye = jnp.where(phase == 1, 1.0, jnp.where(phase == 3, -1.0, 0.0))
                re = re + (one * block_re - eye * block_im)
                im = im + (one * block_im + eye * block_re)
            fields[t, 0, g] = re
            fields[t, 1, g] = im
            return carry

        lax.fori_loop(0, gammas, one_gamma, 0)

    def send_columns(t):
        picked = []
        for c in range(2):
            for g in range(gamma_local):
                value = fields[t, c, gz * gamma_local + g]
                meson_ref[g, t, c] = value
                picked.append(value)
        while len(picked) % nb:
            picked.append(jnp.zeros((rows, 128), jnp.float32))
        for k in range(groups):
            moved = chunk_transpose(picked[k * nb : (k + 1) * nb], rows)
            for j in range(nb):
                outgoing[t, j, :, k * 128 : (k + 1) * 128] = moved[j]
        columns[t, me] = outgoing[t, me]
        copies = []
        for d in range(1, nb):
            there, device = block_peer(d)
            copies.append(send(outgoing.at[t, there], columns.at[t, me], device))
        return copies

    for colour in range(colours):
        multiply(0, colour)
    pl.semaphore_wait(barrier, nb - 1 + nz - 1)
    advance(0)
    for t in range(1, times):
        for colour in range(colours):
            multiply(t, colour)
            if t == 1 and colour == 0:
                advance(0)
        advance(t)
    done = {0: 2}
    for t in range(1, times):
        done[t] = 1
    arriving = {}
    while len(arriving) < times:
        for t in range(times):
            if done[t] < 5:
                advance(t)
                done[t] += 1
            elif t not in arriving:
                make_fields(t)
                arriving[t] = send_columns(t)

    quarter = gammas * rows
    wide = times * width
    rights = []
    for t in range(times):
        for copy in arriving[t]:
            copy.wait_recv()
        rights.append(columns[t].reshape(nb * rows, width))
    right = jnp.concatenate(rights, axis=1)
    row_w = lax.broadcasted_iota(jnp.int32, (quarter, wide), 0)
    lane_w = lax.broadcasted_iota(jnp.int32, (quarter, wide), 1)
    same = (row_w % rows) == (lane_w % rows)
    per = times * 2 * gamma_local
    src_lane = lax.broadcasted_iota(jnp.int32, (wide, 128), 0)
    dst = lax.broadcasted_iota(jnp.int32, (wide, 128), 1) % per
    src_t = src_lane // width
    src_x = (src_lane % width) // rows
    dst_t = dst // (2 * gamma_local)
    dst_x = dst % (2 * gamma_local)
    swapped = (dst_x + gamma_local) % (2 * gamma_local)
    same_t = src_t == dst_t
    straight = jnp.where(same_t & (src_x == dst_x), 1.0, 0.0)
    crossed = jnp.where(
        same_t & (src_x == swapped), jnp.where(dst_x < gamma_local, -1.0, 1.0), 0.0
    )
    picks = (straight, crossed)
    split = max(1, 128 // (per * times))
    while gammas % split or (gammas // split) % 8:
        split -= 1
    part_rows = gammas // split
    out_lane = lax.broadcasted_iota(jnp.int32, (part_rows, 128), 1) // per
    packed = jnp.zeros((part_rows, 128), jnp.float32)
    sums = [[None] * times, [None] * times]
    for t in range(times):
        for c in range(2):
            left = fields[t, c].reshape(quarter, 128)
            cross = jnp.dot(left, right, precision=EXACT, preferred_element_type=jnp.float32)
            cross = jnp.where(same, cross, 0.0)
            sums[c][t] = jnp.sum(cross.reshape(gammas, rows, wide), axis=1)
    total = jnp.dot(
        jnp.concatenate(sums[0], axis=0), straight, precision=EXACT,
        preferred_element_type=jnp.float32,
    ) + jnp.dot(
        jnp.concatenate(sums[1], axis=0), crossed, precision=EXACT,
        preferred_element_type=jnp.float32,
    )
    for t in range(times):
        for h in range(split):
            piece = total[t * gammas + h * part_rows : t * gammas + (h + 1) * part_rows]
            packed = jnp.where(out_lane == h * times + t, piece, packed)
    totals[me] = packed
    copies = []
    for d in range(1, nb):
        _, device = block_peer(d)
        copies.append(send(totals.at[me], totals.at[me], device))
    for copy in copies:
        copy.wait_recv()
    total = totals[0]
    for j in range(1, nb):
        total = total + totals[j]
    trace_ref[...] = total
    for copy in pending:
        copy.wait_send()


def fused(left, right, gamma_cols, gamma_phase, dilution, sizes):
    nx, ny, nz = sizes
    times, spins, parts, colours, modes, depth = left.shape
    nxi = 2 if nx % 2 == 0 else 1
    nxo = nx // nxi
    gammas = gamma_cols.shape[0]
    gamma_local = gammas // nz
    low = modes - dilution.shape[0]
    used = spins * (2 * (spins * low // 128) + 1)
    kz = -(-used // nz)
    rows = modes // (nx * ny)
    nb = nx * ny
    tile = (rows, 128)
    dil = jnp.concatenate([jnp.full((low,), -1, jnp.int32), dilution]).reshape(1, modes)
    dims = (
        times, spins, colours, low, modes, depth, gammas, gamma_local, nz, kz, nxo, nxi, ny, rows,
    )
    scratch = []
    sems = 0
    for t, part, order in flow_list(times):
        k0, k1 = slab_range(part, kz)
        shapes = []
        left_dims = {"gz": nz, "kz": k1 - k0, "outer": nxo, "inner": nxi, "gy": ny}
        for axis in order:
            n = left_dims.pop(axis)
            sems += n - 1
            rest = tuple(left_dims.values())
            shapes.append((max(n - 1, 1),) + rest + tile)
            shapes.append(rest + tile)
        sems += nz - 1
        scratch += [pltpu.VMEM(shape, jnp.float32) for shape in shapes[:7]]
    sems += (times + 1) * (nb - 1)
    groups = -(-(2 * gamma_local) // nb)
    per = times * 2 * gamma_local
    split = max(1, 128 // (per * times))
    while gammas % split or (gammas // split) % 8:
        split -= 1
    block = (times, colours, spins, parts, modes, depth)
    scratch += [
        pltpu.VMEM(block, jnp.bfloat16),
        pltpu.VMEM(block, jnp.bfloat16),
        pltpu.VMEM((times, nz, kz, nxo, nxi, ny) + tile, jnp.float32),
        pltpu.VMEM((times, nz, kz) + tile, jnp.float32),
        pltpu.VMEM((times, spins, spins, 2) + tile, jnp.float32),
        pltpu.VMEM((times, 2, gammas) + tile, jnp.float32),
        pltpu.VMEM((times, nb, rows, groups * 128), jnp.float32),
        pltpu.VMEM((times, nb, rows, groups * 128), jnp.float32),
        pltpu.VMEM((nb, gammas // split, 128), jnp.float32),
        pltpu.SemaphoreType.DMA((2 * times * colours,)),
        pltpu.SemaphoreType.DMA((sems,)),
        pltpu.SemaphoreType.DMA((sems,)),
    ]
    vmem = pl.BlockSpec(memory_space=pltpu.VMEM)
    smem = pl.BlockSpec(memory_space=pltpu.SMEM)
    hbm = pl.BlockSpec(memory_space=pl.ANY)
    meson, packed = pl.pallas_call(
        functools.partial(fused_kernel, dims),
        in_specs=[smem, smem, vmem, hbm, hbm],
        out_specs=[vmem, vmem],
        out_shape=[
            jax.ShapeDtypeStruct((gamma_local, times, 2) + tile, jnp.float32),
            jax.ShapeDtypeStruct((gammas // split, 128), jnp.float32),
        ],
        scratch_shapes=scratch,
        compiler_params=pltpu.CompilerParams(
            collective_id=0, has_side_effects=True, vmem_limit_bytes=60 * 1024 * 1024
        ),
        name="meson_fields",
    )(gamma_cols, gamma_phase, dil, left, right)
    grid = packed[:, : split * times * per]
    grid = grid.reshape(gammas // split, split, times, times, 2, gamma_local)
    return meson, jnp.transpose(grid, (2, 3, 5, 1, 0, 4)).reshape(
        times, times, gamma_local, gammas, 2
    )


def local(sizes, left_modes, right_modes, gamma_cols, gamma_phase, dilution, time_pairs):
    left = jnp.transpose(left_modes, (0, 1, 2, 4, 3, 5))
    right = jnp.transpose(right_modes, (0, 1, 2, 4, 3, 5))
    times = left.shape[0]
    modes = left.shape[4]
    meson_fields, grid = fused(left, right, gamma_cols, gamma_phase, dilution, sizes)
    time_ids = jnp.arange(times, dtype=jnp.int32)
    first = time_pairs[:, 0:1] == time_ids[None, :]
    second = time_pairs[:, 1:2] == time_ids[None, :]
    keep = second[:, :, None] & first[:, None, :]
    chosen = jnp.where(keep[:, :, :, None, None, None], grid[None], 0.0)
    traces = jnp.sum(chosen, axis=(1, 2)) / modes
    return (meson_fields, traces)


def solution(mesh):
    sizes = (mesh.shape["gx"], mesh.shape["gy"], mesh.shape["gz"])
    modes_spec = P(None, None, None, None, None, ("gx", "gy", "gz"))
    return jax.shard_map(
        functools.partial(local, sizes),
        mesh=mesh,
        in_specs=(modes_spec, modes_spec, P(), P(), P(), P()),
        out_specs=(P("gz", None, None, ("gx", "gy"), None), P(None, "gz", None, None)),
        check_vma=False,
    )
```

time: 60 us -> 56.2 us (0.937)
  Pallas kernels: 55.6 us -> 47.7 us
  local copies, waits for them, and re-layouts: 2.5 us -> 7.2 us
  other arithmetic: 0.92 us -> 0.25 us
    pallas_call x2 -> x1, Pallas kernels: 55.6 us -> 47.7 us  [fused(): pl.pallas_call(functools.partial(fused_kernel, dims), in_specs=[smem, sme...]
    unnamed x10 -> x6, local copies, waits for them, and re-layouts: 1.47 us -> 4.91 us
    reshape x1 -> x3, local copies, waits for them, and re-layouts: 0.07 us -> 2.18 us  [the longest x1 1.26 us: fused(): jnp.concatenate([jnp.full((low,), -1, jnp.int32), dilution])]
    eq x1 -> x0, local copies, waits for them, and re-layouts: 0.76 us -> none  [local(): first = time_pairs[:, 0:1] == time_ids[None, :]]
    convert_element_type x1 -> x0, other arithmetic: 0.66 us -> none  [local_blocks(): (dilution[None, :] == jnp.arange(spins, dtype=jnp.int32)[:, None]).astype...]
where the time goes in v2:
time: 56.2 us; the launch traced here: 55.9 us
  Pallas kernels  47.7 us (85%)
  local copies, waits for them, and re-layouts  7.2 us (13%)
  between operations  0.67 us (1%)
    pallas_call x1, Pallas kernels, fused(): pl.pallas_call(functools.partial(fused_kernel, dims), in_specs=[smem, sme...  47.7 us
    unnamed x6, local copies, waits for them, and re-layouts  4.91 us
    reshape x1, local copies, waits for them, and re-layouts, fused(): jnp.concatenate([jnp.full((low,), -1, jnp.int32), dilution])  1.26 us

profile of v2, /device:TPU:0, one launch (start us, length us, event | category | flops | bytes accessed | tf_op | source)
XLA Modules:
  0.0 55.9 jit_solution(10483689825257803095)
XLA Ops:
  0.6 1.4 %copy.14.cols_ref = s32[16,4]{1,0:T(8,128)} copy(s32[16,4]{0,1:T(4,128)} %param.8) | data formatting | bytes 512 | tf_op args[2]
  2.0 1.4 %copy.15.phase_ref = s32[16,4]{1,0:T(8,128)} copy(s32[16,4]{0,1:T(4,128)} %param.9) | data formatting | bytes 512 | tf_op args[3]
  3.3 1.3 %pad_bitcast_fusion.dil_ref = s32[1,128]{1,0:T(1,128)} fusion(s32[64]{0:T(128)} %param.10), kind=kLoop, calls=%fused_computation.7 | loop fusion | bytes 768 | tf_op jit(solution)/shard_map/reshape | solution.py:391
  4.6 0.0 copy-start
  4.6 47.7 %meson_fields.1 = (f32[8,2,2,8,128]{4,3,2,1,0:T(8,128)}, f32[8,128]{1,0:T(8,128)}) custom-call(s32[16,4]{1,0:T(8,128)} %copy.14.cols_ref, s32[16,4]{1,0:T(8,128)} %copy.15.phase_ref, s32[1,128]{1,0:T(1,128)} %pad_bitcast_fusion.dil_ref, bf16[2,4,2,3,128,512]{5,4,3,2,1,0:T(8,128)(2,1)} %bitcast.11, bf16[2,4,2,3,128,512]{5,4,3,2,1,0:T(8,128)(2,1)} %bitcast.12), custom_call_target="tpu_custom_call" | custom-call | tf_op jit(solution)/shard_map/meson_fields/pallas_call | solution.py:433
  52.4 0.8 %reshape.53 = f32[8,2,2,2,2,8]{5,4,3,2,1,0:T(2,128)S(1)} reshape(f32[8,128]{1,0:T(8,128)} %get-tuple-element.5) | data formatting | bytes 8192 | tf_op jit(solution)/shard_map/reshape | solution.py:448
  53.2 0.1 copy.16
  53.3 0.1 broadcast_in_dim.29
  53.4 0.0 copy-done
  53.4 0.1 iota_compare_fusion
  53.5 0.1 broadcast_and_fusion
  53.6 0.1 select_reduce_fusion
  53.7 0.6 %copy.17 = f32[4,8,16,2]{2,3,1,0:T(2,128)} copy(f32[4,8,16,2]{2,1,3,0:T(8,128)S(1)} %broadcast_multiply_fusion) | data formatting | bytes 8192
  54.3 1.6 %copy.19 = f32[8,2,2,8,128]{4,3,2,1,0:T(8,128)} copy(f32[8,2,2,8,128]{4,3,2,1,0:T(8,128)} %get-tuple-element.14) | data formatting | bytes 262144
  (2 shorter events, 0.0 us)
Async XLA Ops:
  4.6 48.8 %copy-start = (s32[4,2]{0,1:T(2,128)S(1)}, s32[4,2]{0,1:T(2,128)}, u32[]{:S(2)}) copy-start(s32[4,2]{0,1:T(2,128)} %param.11) | copy-start | bytes 100

commit v3 on v2

--- a/solution.py
+++ b/solution.py
@@ -10,6 +10,11 @@
 EXACT = lax.Precision.HIGHEST
 MESH = pl.DeviceIdType.MESH
 NT = (((1,), (1,)), ((), ()))
+
+
+TAIL = 5
+CUTS0 = (0, 1, 3)
+CUTS1 = (0, 1, 3)
 
 
 def nt_dot(a, b):
@@ -35,24 +40,22 @@
     return rows
 
 
-def flow_list(times):
-    flows = []
-    for t in range(times):
-        flows.append((t, 0, ("inner", "outer", "gz", "gy")))
-        flows.append((t, 1, ("inner", "gz", "outer", "gy")))
-    return flows
-
-
-def slab_range(part, kz):
-    cut = kz // 2
-    return (0, cut) if part == 0 else (cut, kz)
+def flow_list(times, kz):
+    tail = kz // TAIL if TAIL else 0
+    cut = (kz - tail + 1) // 2
+    orders = (
+        (0, cut, ("inner", "outer", "gz", "gy")),
+        (cut, kz - tail, ("inner", "gz", "outer", "gy")),
+        (kz - tail, kz, ("inner", "gy", "outer", "gz")),
+    )
+    return [(t,) + flow for t in range(times) for flow in orders if flow[0] < flow[1]]
 
 
 def fused_kernel(
-    dims, cols_ref, phase_ref, dil_ref, left_ref, right_ref, meson_ref, trace_ref, *scratch
+    dims, cols_ref, phase_ref, pairs_ref, dil_ref, left_ref, right_ref, meson_ref, trace_ref, *scratch
 ):
     (times, spins, colours, low, modes, depth, gammas, gamma_local, nz, kz, nxo, nxi, ny, rows) = dims
-    flow_specs = flow_list(times)
+    flow_specs = flow_list(times, kz)
     bufs = scratch[: 7 * len(flow_specs)]
     (
         left_buf, right_buf, parts, gathered, blocks, fields, outgoing, columns, totals,
@@ -94,32 +97,54 @@
         )
 
     noise_count = modes - low
+    at_lane = lax.broadcasted_iota(jnp.int32, (noise_count, noise_count), 1)
+    at_row = lax.broadcasted_iota(jnp.int32, (noise_count, noise_count), 0)
+    dil_row = jnp.broadcast_to(dil_ref[...], (noise_count, noise_count)).astype(jnp.float32)
+    dil_col = jnp.sum(jnp.where(at_lane == at_row, dil_row, 0.0), axis=1, keepdims=True)
+    masks = []
+    for r in range(spins):
+        column = jnp.where(dil_col == r, 1.0, 0.0)
+        masks.append(jnp.broadcast_to(column, (noise_count, depth)).astype(jnp.bfloat16))
     at_lane = lax.broadcasted_iota(jnp.int32, (noise_count, modes), 1)
     at_row = lax.broadcasted_iota(jnp.int32, (noise_count, modes), 0)
-    dil_row = jnp.broadcast_to(dil_ref[...], (noise_count, modes))
-    masks = []
-    for r in range(spins):
-        hit = jnp.where((at_lane == at_row + low) & (dil_row == r), 1.0, 0.0)
-        column = jnp.sum(hit, axis=1, keepdims=True)
-        masks.append(jnp.broadcast_to(column, (noise_count, depth)).astype(jnp.bfloat16))
+    spread = jnp.where(at_lane == at_row + low, jnp.broadcast_to(dil_col, (noise_count, modes)), 0.0)
+    dil_lanes = jnp.sum(spread, axis=0, keepdims=True)
 
     half = spins * low // 128
     per_spin = 2 * half + 1
 
-    def multiply(t, colour):
-        for copy in loads[t * colours + colour]:
-            copy.wait()
-        left = left_buf.at[t, colour]
-        right = right_buf.at[t, colour]
-        left_re = left[:, 0].reshape(spins * modes, depth)
-        left_im = left[:, 1].reshape(spins * modes, depth)
-        low_re = jnp.concatenate([right[r, 0, :low] for r in range(spins)], axis=0)
-        low_im = jnp.concatenate([right[r, 1, :low] for r in range(spins)], axis=0)
-        noise_re = right[0, 0, low:] * masks[0]
-        noise_im = right[0, 1, low:] * masks[0]
-        for r in range(1, spins):
-            noise_re = noise_re + right[r, 0, low:] * masks[r]
-            noise_im = noise_im + right[r, 1, low:] * masks[r]
+    def multiply(t, first, end):
+        for colour in range(first, end):
+            for copy in loads[t * colours + colour]:
+                copy.wait()
+        span = range(first, end)
+
+        def left(c):
+            return jnp.concatenate(
+                [left_buf[t, k, :, c].reshape(spins * modes, depth) for k in span], axis=1
+            )
+
+        def right_low(c):
+            return jnp.concatenate(
+                [
+                    jnp.concatenate([right_buf[t, k, r, c, :low] for r in range(spins)], axis=0)
+                    for k in span
+                ],
+                axis=1,
+            )
+
+        def right_noise(c):
+            chosen = []
+            for k in span:
+                value = right_buf[t, k, 0, c, low:] * masks[0]
+                for r in range(1, spins):
+                    value = value + right_buf[t, k, r, c, low:] * masks[r]
+                chosen.append(value)
+            return jnp.concatenate(chosen, axis=1)
+
+        left_re, left_im = left(0), left(1)
+        low_re, low_im = right_low(0), right_low(1)
+        noise_re, noise_im = right_noise(0), right_noise(1)
         low_out_re = nt_dot(left_re, low_re) + nt_dot(left_im, low_im)
         low_out_im = nt_dot(left_re, low_im) + nt_dot(left_im, -low_re)
         noise_out = nt_dot(left_re, jnp.concatenate([noise_re, noise_im], axis=0)) + nt_dot(
@@ -128,7 +153,7 @@
 
         def put(k, piece):
             piece = piece.reshape(nxo, nxi, ny, rows, 128)
-            if colour == 0:
+            if first == 0:
                 parts[t, k // kz, k % kz] = piece
             else:
                 parts[t, k // kz, k % kz] += piece
@@ -139,7 +164,7 @@
                 put(s * per_spin + k, low_out_re[at, k * 128 : (k + 1) * 128])
                 put(s * per_spin + half + k, low_out_im[at, k * 128 : (k + 1) * 128])
             put(s * per_spin + 2 * half, noise_out[at])
-        if colour == 0:
+        if first == 0:
             for k in range(spins * per_spin, nz * kz):
                 parts[t, k // kz, k % kz] = jnp.zeros((nxo, nxi, ny, rows, 128), jnp.float32)
 
@@ -201,8 +226,7 @@
         flow["step"] = step + 1
 
     flows = []
-    for n, (t, part, order) in enumerate(flow_specs):
-        k0, k1 = slab_range(part, kz)
+    for n, (t, k0, k1, order) in enumerate(flow_specs):
         flows.append({
             "t": t, "k0": k0, "k1": k1, "order": order, "step": 0,
             "src": parts.at[t, :, k0:k1],
@@ -224,7 +248,7 @@
 
     lane = lax.broadcasted_iota(jnp.int32, (rows, 128), 1)
     is_low = lane < low
-    dil = jnp.broadcast_to(dil_ref[...], (rows, 128))
+    dil = jnp.broadcast_to(dil_lanes, (rows, 128))
     pack = 128 // low
     groups = -(-(2 * gamma_local) // nb)
     width = groups * 128
@@ -254,8 +278,8 @@
             re = jnp.zeros((rows, 128), jnp.float32)
             im = jnp.zeros((rows, 128), jnp.float32)
             for s in range(spins):
-                col = cols_ref[g, s]
-                phase = phase_ref[g, s]
+                col = cols_ref[s, g]
+                phase = phase_ref[s, g]
                 block_re = blocks[t, s, col, 0]
                 block_im = blocks[t, s, col, 1]
                 one = jnp.where(phase == 0, 1.0, jnp.where(phase == 2, -1.0, 0.0))
@@ -288,14 +312,14 @@
             copies.append(send(outgoing.at[t, there], columns.at[t, me], device))
         return copies
 
-    for colour in range(colours):
-        multiply(0, colour)
+    for k in range(len(CUTS0) - 1):
+        multiply(0, CUTS0[k] * colours // 3, CUTS0[k + 1] * colours // 3)
     pl.semaphore_wait(barrier, nb - 1 + nz - 1)
     advance(0)
     for t in range(1, times):
-        for colour in range(colours):
-            multiply(t, colour)
-            if t == 1 and colour == 0:
+        for k in range(len(CUTS1) - 1):
+            multiply(t, CUTS1[k] * colours // 3, CUTS1[k + 1] * colours // 3)
+            if t == 1 and k == 0:
                 advance(0)
         advance(t)
     done = {0: 2}
@@ -370,12 +394,24 @@
     total = totals[0]
     for j in range(1, nb):
         total = total + totals[j]
-    trace_ref[...] = total
+    turned = jnp.transpose(total)
+    span = times * per
+    grid = jnp.concatenate([turned[h * span : (h + 1) * span] for h in range(split)], axis=1)
+    for p in range(pairs_ref.shape[1]):
+        first, second = pairs_ref[0, p], pairs_ref[1, p]
+        for c in range(2):
+            value = jnp.zeros((gamma_local, gammas), jnp.float32)
+            for t_h in range(times):
+                for t_g in range(times):
+                    at = ((t_h * times + t_g) * 2 + c) * gamma_local
+                    keep = (first == t_g) & (second == t_h)
+                    value = value + jnp.where(keep, grid[at : at + gamma_local], 0.0)
+            trace_ref[p, c] = value / modes
     for copy in pending:
         copy.wait_send()
 
 
-def fused(left, right, gamma_cols, gamma_phase, dilution, sizes):
+def fused(left, right, gamma_cols, gamma_phase, dilution, time_pairs, sizes):
     nx, ny, nz = sizes
     times, spins, parts, colours, modes, depth = left.shape
     nxi = 2 if nx % 2 == 0 else 1
@@ -388,14 +424,12 @@
     rows = modes // (nx * ny)
     nb = nx * ny
     tile = (rows, 128)
-    dil = jnp.concatenate([jnp.full((low,), -1, jnp.int32), dilution]).reshape(1, modes)
     dims = (
         times, spins, colours, low, modes, depth, gammas, gamma_local, nz, kz, nxo, nxi, ny, rows,
     )
     scratch = []
     sems = 0
-    for t, part, order in flow_list(times):
-        k0, k1 = slab_range(part, kz)
+    for t, k0, k1, order in flow_list(times, kz):
         shapes = []
         left_dims = {"gz": nz, "kz": k1 - k0, "outer": nxo, "inner": nxi, "gy": ny}
         for axis in order:
@@ -430,40 +464,29 @@
     vmem = pl.BlockSpec(memory_space=pltpu.VMEM)
     smem = pl.BlockSpec(memory_space=pltpu.SMEM)
     hbm = pl.BlockSpec(memory_space=pl.ANY)
-    meson, packed = pl.pallas_call(
+    return pl.pallas_call(
         functools.partial(fused_kernel, dims),
-        in_specs=[smem, smem, vmem, hbm, hbm],
+        in_specs=[smem, smem, smem, vmem, hbm, hbm],
         out_specs=[vmem, vmem],
         out_shape=[
             jax.ShapeDtypeStruct((gamma_local, times, 2) + tile, jnp.float32),
-            jax.ShapeDtypeStruct((gammas // split, 128), jnp.float32),
+            jax.ShapeDtypeStruct((time_pairs.shape[0], 2, gamma_local, gammas), jnp.float32),
         ],
         scratch_shapes=scratch,
         compiler_params=pltpu.CompilerParams(
-            collective_id=0, has_side_effects=True, vmem_limit_bytes=60 * 1024 * 1024
+            collective_id=0, has_side_effects=True, vmem_limit_bytes=54 * 1024 * 1024
         ),
         name="meson_fields",
-    )(gamma_cols, gamma_phase, dil, left, right)
-    grid = packed[:, : split * times * per]
-    grid = grid.reshape(gammas // split, split, times, times, 2, gamma_local)
-    return meson, jnp.transpose(grid, (2, 3, 5, 1, 0, 4)).reshape(
-        times, times, gamma_local, gammas, 2
-    )
+    )(gamma_cols.T, gamma_phase.T, time_pairs.T, dilution.reshape(1, -1), left, right)
 
 
 def local(sizes, left_modes, right_modes, gamma_cols, gamma_phase, dilution, time_pairs):
     left = jnp.transpose(left_modes, (0, 1, 2, 4, 3, 5))
     right = jnp.transpose(right_modes, (0, 1, 2, 4, 3, 5))
-    times = left.shape[0]
-    modes = left.shape[4]
-    meson_fields, grid = fused(left, right, gamma_cols, gamma_phase, dilution, sizes)
-    time_ids = jnp.arange(times, dtype=jnp.int32)
-    first = time_pairs[:, 0:1] == time_ids[None, :]
-    second = time_pairs[:, 1:2] == time_ids[None, :]
-    keep = second[:, :, None] & first[:, None, :]
-    chosen = jnp.where(keep[:, :, :, None, None, None], grid[None], 0.0)
-    traces = jnp.sum(chosen, axis=(1, 2)) / modes
-    return (meson_fields, traces)
+    meson_fields, traces = fused(
+        left, right, gamma_cols, gamma_phase, dilution, time_pairs, sizes
+    )
+    return (meson_fields, jnp.transpose(traces, (0, 2, 3, 1)))
 
 
 def solution(mesh):

time: 56.2 us -> 49.3 us (0.88)
  local copies, waits for them, and re-layouts: 7.2 us -> 2.96 us
  Pallas kernels: 47.7 us -> 45.5 us
    pallas_call x1, Pallas kernels: 47.7 us -> 45.5 us  [fused(): pl.pallas_call(functools.partial(fused_kernel, dims), in_specs=[smem, sme...]
    reshape x3 -> x0, local copies, waits for them, and re-layouts: 2.18 us -> none  [the longest x1 1.26 us: fused(): jnp.concatenate([jnp.full((low,), -1, jnp.int32), dilution])]
    unnamed x6 -> x2, local copies, waits for them, and re-layouts: 4.91 us -> 2.96 us
where the time goes in v3:
time: 49.3 us; the launch traced here: 49.1 us
  Pallas kernels  45.5 us (92%)
  local copies, waits for them, and re-layouts  2.96 us (6%)
  between operations  0.64 us (1%)
    pallas_call x1, Pallas kernels, fused(): pl.pallas_call(functools.partial(fused_kernel, dims), in_specs=[smem, sme...  45.5 us
    unnamed x2, local copies, waits for them, and re-layouts  2.96 us

profile of v3, /device:TPU:0, one launch (start us, length us, event | category | flops | bytes accessed | tf_op | source)
XLA Modules:
  0.0 49.1 jit_solution(484890123035964957)
XLA Ops:
  0.6 45.5 %meson_fields.1 = (f32[8,2,2,8,128]{4,3,2,1,0:T(8,128)}, f32[4,2,8,16]{3,2,1,0:T(8,128)}) custom-call(s32[4,16]{1,0:T(4,128)} %bitcast.10, s32[4,16]{1,0:T(4,128)} %bitcast.11, s32[2,4]{1,0:T(2,128)} %bitcast.12, s32[1,64]{1,0:T(1,128)} %bitcast.13, bf16[2,4,2,3,128,512]{5,4,3,2,1,0:T(8,128)(2,1)} %bitcast.7, bf16[2,4,2,3,128,512]{5,4,3,2,1,0:T(8,128)(2,1)} %bitcast.8), custom_call_target="tpu_custom_call" | custom-call | tf_op jit(solution)/shard_map/meson_fields/pallas_call | solution.py:467
  46.1 1.4 %copy.8 = f32[4,8,16,2]{2,3,1,0:T(2,128)} copy(f32[4,8,16,2]{2,1,3,0:T(8,128)} %bitcast.9) | data formatting | bytes 8192
  47.5 1.6 %copy.10 = f32[8,2,2,8,128]{4,3,2,1,0:T(8,128)} copy(f32[8,2,2,8,128]{4,3,2,1,0:T(8,128)} %get-tuple-element.10) | data formatting | bytes 262144
